TPU v7x, 32 devices: a whole 2x2x4 slice. The times are simulated.
32 devices in a mesh: ctx: 8 (over z, y), grp: 4 (over x, core).
Axes of the slice: x: 2, y: 2, z: 4, core: 2. Of those that a mesh axis runs over, the one named last changes fastest.
Arguments:
- q_latent: bfloat16 [2048, 1536], P('ctx'), may hold values from -210 to 210
- kv_latent: bfloat16 [2048, 576], P('ctx'), may hold values from -6 to 6
- kv_gain: float32 [512], replicated, may hold values from 0.1 to 1.9
- q_weight: bfloat16 [1536, 6144], P('ctx', 'grp'), may hold values from -0.15625 to 0.15625
- kv_weight: bfloat16 [512, 8192], P('ctx', 'grp'), may hold values from -0.25 to 0.25
- out_weight: bfloat16 [4096, 7168], P('grp', 'ctx'), may hold values from -0.125 to 0.125
- documents: int32 [2048], replicated, may hold values from 0 to 3, never falling along the last dimension, each value on 1 to 1024 neighbouring positions
Outputs:
- mixed: bfloat16 [2048, 7168], P('ctx', 'grp')
All inputs are finite; a program needn't handle non-finite values.
Results may differ from a plain program's by a relative error of at most 0.018.
Values may be sent and summed in bfloat16 or wider, within the bound.
No kernel may reach another device: no remote copies, remote signals or barrier semaphores. Data moves between devices by JAX's collectives and lax.ppermute only.
A program may use at most 64 MiB of HBM per device.

v0:
```python
import jax
import jax.numpy as jnp
from jax import lax
from jax.sharding import PartitionSpec as P

KL = 512
NOPE = 128
ROPE = 64
VDIM = 128


epsilon = 1e-06


def shifted(block, axis, distance):
    devices = range(lax.axis_size(axis))
    route = [(i - distance, i) for i in devices if i - distance in devices]
    return lax.ppermute(block, axis, route)


def rotate(inputs, positions):
    half_width = inputs.shape[-1] // 2
    inverse = 10000.0 ** (-2.0 * jnp.arange(half_width, dtype=jnp.float32) / inputs.shape[-1])
    angles = positions.astype(jnp.float32)[:, None] * inverse[None, :]
    shape = (angles.shape[0],) + (1,) * (inputs.ndim - 2) + (half_width,)
    cosine = jnp.cos(angles).reshape(shape)
    sine_part = jnp.sin(angles).reshape(shape)
    front_half = inputs[..., :half_width]
    back_half = inputs[..., half_width:]
    return jnp.concatenate(
        [front_half * cosine - back_half * sine_part, back_half * cosine + front_half * sine_part],
        axis=-1,
    )


def prepare(latent_block, positions, kv_gain):
    latent = latent_block[:, :KL].astype(jnp.float32)
    normed = (
        latent * lax.rsqrt(jnp.mean(latent * latent, axis=-1, keepdims=True) + epsilon) * kv_gain
    )
    key_rope = rotate(latent_block[:, KL:].astype(jnp.float32), positions).astype(jnp.bfloat16)
    return (normed.astype(jnp.bfloat16), key_rope)


def folder(left, weight_piece):
    return jnp.dot(left, weight_piece, preferred_element_type=jnp.float32)


def per_device(q_latent, kv_latent, kv_gain, q_weight, kv_weight, out_weight, documents):
    rows_dev = q_latent.shape[0]
    head_count = q_weight.shape[1] // (NOPE + ROPE)
    block_index = lax.axis_index("ctx")
    query_pos = block_index * rows_dev + jnp.arange(rows_dev, dtype=jnp.int32)
    prior_pos = query_pos - rows_dev
    query_full = folder(q_latent, lax.all_gather(q_weight, "ctx", axis=0, tiled=True))
    query_full = query_full.reshape(rows_dev, head_count, NOPE + ROPE)
    query_nope = query_full[..., :NOPE].astype(jnp.bfloat16)
    query_rope = rotate(query_full[..., NOPE:], query_pos).astype(jnp.bfloat16)
    previous = shifted(kv_latent, "ctx", 1)
    latent_block = jnp.concatenate([previous, kv_latent], axis=0)
    positions = jnp.concatenate([prior_pos, query_pos])
    normed, key_rope = prepare(latent_block, positions, kv_gain)
    key_value = folder(normed, lax.all_gather(kv_weight, "ctx", axis=0, tiled=True))
    key_value = key_value.astype(jnp.bfloat16)
    key_value = key_value.reshape(2 * rows_dev, head_count, NOPE + VDIM)
    key_nope = key_value[..., :NOPE]
    values = key_value[..., NOPE:]
    key_pos = jnp.concatenate([prior_pos, query_pos])
    query_docs = lax.dynamic_slice_in_dim(documents, block_index * rows_dev, rows_dev, 0)
    prior_docs = lax.dynamic_slice_in_dim(
        documents, jnp.maximum(block_index - 1, 0) * rows_dev, rows_dev, 0
    )
    key_docs = jnp.concatenate([prior_docs, query_docs])
    allowed = (
        (key_docs[None, :] == query_docs[:, None])
        & (key_pos[None, :] <= query_pos[:, None])
        & (key_pos[None, :] >= 0)
    )
    scale = (NOPE + ROPE) ** (-0.5)
    scores = jnp.einsum("qhd,khd->hqk", query_nope, key_nope, preferred_element_type=jnp.float32)
    scores = (
        scores + jnp.einsum("qhr,kr->hqk", query_rope, key_rope, preferred_element_type=jnp.float32)
    ) * scale
    scores = jnp.where(allowed[None], scores, -1e30)
    highest = jnp.max(scores, axis=-1, keepdims=True)
    weights = jnp.exp(scores - highest)
    probs = (weights / jnp.sum(weights, axis=-1, keepdims=True)).astype(jnp.bfloat16)
    attended = jnp.einsum("hqk,khv->qhv", probs, values, preferred_element_type=jnp.float32).astype(
        jnp.bfloat16
    )
    attended = attended.reshape(rows_dev, head_count * VDIM)
    partial_value = jnp.dot(
        attended,
        lax.all_gather(out_weight, "ctx", axis=1, tiled=True),
        preferred_element_type=jnp.float32,
    )
    mixed = lax.psum_scatter(
        partial_value.astype(jnp.bfloat16), "grp", scatter_dimension=1, tiled=True
    )
    return mixed


def solution(mesh):
    placed = (
        P("ctx", None),
        P("ctx", None),
        P(),
        P("ctx", "grp"),
        P("ctx", "grp"),
        P("grp", "ctx"),
        P(),
    )
    return jax.shard_map(
        per_device, mesh=mesh, in_specs=placed, out_specs=P("ctx", "grp"), check_vma=False
    )
```

profile of v0, /device:TPU:0, one launch (start us, length us, event | category | flops | bytes accessed | tf_op | source)
XLA Modules:
  0.0 400.4 jit_solution(10570388636576462682)
XLA Ops:
  6.5 0.7 all-gather.4.cloned.1.call-update
  7.3 0.7 all-gather.6.cloned.1.call-update
  8.1 0.7 all-gather.8.cloned.1.call-update
  8.8 4.9 %collective-permute-start = (bf16[256,576]{0,1:T(8,128)(2,1)}, bf16[256,576]{0,1:T(8,128)(2,1)S(1)}, u32[]{:S(2)}, u32[]{:S(2)}) collective-permute-start(bf16[256,576]{0,1:T(8,128)(2,1)} %param.8), channel_id=1, source_target_pairs={{0,4},{4,8},{8,12},{12,16},{16,20},{20,24},{24,28},{1,5},{5,9},{9,... | collective-permute-start | bytes 884744 | tf_op jit(solution)/shard_map/ppermute | solution.py:18
  13.8 0.8 fusion.34
  14.6 0.2 multiply_cosine_fusion.1
  14.8 0.2 and_and_fusion
  15.0 5.2 %collective-permute-done = bf16[256,576]{0,1:T(8,128)(2,1)S(1)} collective-permute-done((bf16[256,576]{0,1:T(8,128)(2,1)}, bf16[256,576]{0,1:T(8,128)(2,1)S(1)}, u32[]{:S(2)}, u32[]{:S(2)}) %collective-permute-start) | collective-permute-done | bytes 294944 | tf_op jit(solution)/shard_map/ppermute | solution.py:18
  20.3 1.0 constant_dynamic-update-slice_fusion
  21.3 0.2 fusion.5
  21.5 0.3 fusion.23
  21.8 39.5 %all-gather.4.cloned.1.call-done = bf16[512,2048]{1,0:T(8,128)(2,1)} async-done(((bf16[64,2048]{1,0:T(8,128)(2,1)}), bf16[512,2048]{1,0:T(8,128)(2,1)}) %all-gather.4.cloned.1.call-update) | async-done | bytes 2097168 | tf_op jit(solution)/shard_map/all_gather | solution.py:63
  61.3 3.0 convolution_convert_fusion.1
  64.3 0.7 copy.29
  65.1 76.3 %all-gather.6.cloned.1.call-done = bf16[1536,1536]{1,0:T(8,128)(2,1)} async-done(((bf16[192,1536]{1,0:T(8,128)(2,1)}), bf16[1536,1536]{1,0:T(8,128)(2,1)}) %all-gather.6.cloned.1.call-update) | async-done | bytes 4718608 | tf_op jit(solution)/shard_map/all_gather | solution.py:55
  141.4 4.3 %fusion.36 = f32[256,1536]{0,1:T(8,128)S(1)} fusion(bf16[256,1536]{1,0:T(8,128)(2,1)S(1)} %copy-done, bf16[1536,1536]{1,0:T(8,128)(2,1)} %all-gather.6.cloned.1.call-done), kind=kOutput, calls=%fused_computation.60 | convolution fusion | flops 1207959552 | bytes 7077888 | tf_op jit(solution)/shard_map/dot_general | solution.py:46
  145.7 0.8 fusion.8
  146.5 1.0 fusion.2
  147.5 2.0 copy-done.1
  149.5 1.7 fusion.35
  151.2 8.3 %fusion.4 = bf16[8,128,256]{2,1,0:T(8,128)(2,1)S(1)} fusion(f32[8,256]{1,0:T(8,128)S(1)} %fusion.35, bf16[512,8,128]{2,1,0:T(8,128)(2,1)S(1)} %get-tuple-element.5, f32[8,256,512]{2,1,0:T(8,128)} %copy-done.1), kind=kOutput, calls=%fused_computation.11 | convolution fusion | flops 271845888 | bytes 5775360 | tf_op jit(solution)/shard_map/hqk,khv->qhv/dot_general | solution.py:88
  159.5 184.1 %all-gather.8.cloned.1.call-done = bf16[1024,7168]{1,0:T(8,128)(2,1)} async-done(((bf16[1024,896]{1,0:T(8,128)(2,1)}), bf16[1024,7168]{1,0:T(8,128)(2,1)}) %all-gather.8.cloned.1.call-update) | async-done | bytes 14680080 | tf_op jit(solution)/shard_map/all_gather | solution.py:94
  343.6 10.8 %convolution_convert_fusion = bf16[256,7168]{1,0:T(8,128)(2,1)} fusion(bf16[256,1024]{0,1:T(8,128)(2,1)S(1)} %bitcast.26, bf16[1024,7168]{1,0:T(8,128)(2,1)} %all-gather.8.cloned.1.call-done), kind=kOutput, calls=%fused_computation.1 | convolution fusion | flops 3759931392 | bytes 18874368 | tf_op jit(solution)/shard_map/dot_general | solution.py:92
  354.4 39.4 %reduce-scatter.2.cloned.1.call-done = bf16[256,1792]{1,0:T(8,128)(2,1)} async-done(((bf16[256,7168]{1,0:T(8,128)(2,1)}), bf16[256,1792]{1,0:T(8,128)(2,1)}) %reduce-scatter.2.cloned.1.call-update) | async-done | bytes 917520 | tf_op jit(solution)/shard_map/reduce_scatter | solution.py:97
  (21 shorter events, 0.4 us)
Async XLA Ops:
  6.5 134.8 %copy-start = (bf16[256,1536]{1,0:T(8,128)(2,1)S(1)}, bf16[256,1536]{1,0:T(8,128)(2,1)}, u32[]{:S(2)}) copy-start(bf16[256,1536]{1,0:T(8,128)(2,1)} %param.7) | copy-start | bytes 2359300
  6.5 54.8 %copy-start.2 = (f32[512]{0:T(512)S(1)}, f32[512]{0:T(512)}, u32[]{:S(2)}) copy-start(f32[512]{0:T(512)} %param.9) | copy-start | bytes 6148
  6.5 54.8 %all-gather.4.cloned.1.call-start = ((), (), s32[]{:S(2)}) async-start(), calls=%async_computation.1 | async-start | bytes 2359296 | tf_op jit(solution)/shard_map/all_gather | solution.py:63
  7.3 134.1 %all-gather.6.cloned.1.call-start = ((), (), s32[]{:S(2)}) async-start(), calls=%async_computation.2 | async-start | bytes 5308416 | tf_op jit(solution)/shard_map/all_gather | solution.py:55
  8.0 335.6 %all-gather.8.cloned.1.call-start = ((), (), s32[]{:S(2)}) async-start(), calls=%async_computation.3 | async-start | bytes 16515072 | tf_op jit(solution)/shard_map/all_gather | solution.py:94
  8.7 385.1 %reduce-scatter.2.cloned.1.call-start = ((), (), s32[]{:S(2)}) async-start(), calls=%async_computation.4 | async-start | bytes 4587520 | tf_op jit(solution)/shard_map/reduce_scatter | solution.py:97
  8.8 11.5 %collective-permute-start = (bf16[256,576]{0,1:T(8,128)(2,1)}, bf16[256,576]{0,1:T(8,128)(2,1)S(1)}, u32[]{:S(2)}, u32[]{:S(2)}) collective-permute-start(bf16[256,576]{0,1:T(8,128)(2,1)} %param.8), channel_id=1, source_target_pairs={{0,4},{4,8},{8,12},{12,16},{16,20},{20,24},{24,28},{1,5},{5,9},{9,... | collective-permute-start | bytes 884744 | tf_op jit(solution)/shard_map/ppermute | solution.py:18
  147.5 2.0 copy-start.1
Sparse Core Ops, SparseCore 0:
  9.5 51.7 all-gather.3
  63.5 77.8 all-gather.5
  143.6 199.9 all-gather.7
  354.5 39.2 reduce-scatter.1
where the time goes:
time: 401 us; the launch traced here: 400 us
  waiting for transfers between devices  347 us (87%)
  matrix products  28 us (7%)
  between operations  13.3 us (3%)
  starting transfers between devices  5.04 us (1%)
  local copies, waits for them, and re-layouts  4.66 us (1%)
    all_gather x1, waiting for transfers between devices, per_device(): lax.all_gather(out_weight, 'ctx', axis=1, tiled=True)  184 us
    all_gather x1, waiting for transfers between devices, per_device(): lax.all_gather(q_weight, 'ctx', axis=0, tiled=True)  76.3 us
    all_gather x1, waiting for transfers between devices, per_device(): lax.all_gather(kv_weight, 'ctx', axis=0, tiled=True)  39.5 us
    reduce_scatter x1, waiting for transfers between devices, per_device(): lax.psum_scatter(partial_value.astype(jnp.bfloat16), 'grp', scatter_dimen...  39.4 us
    dot_general x1, matrix products, per_device(): jnp.dot(attended, lax.all_gather(out_weight, 'ctx', axis=1, tiled=True),...  10.8 us
    dot_general x1, matrix products, per_device(): jnp.einsum('hqk,khv->qhv', probs, values, preferred_element_type=jnp.floa...  8.25 us
  transfers between devices with their start and end apart: 5, of which 5 were waited for; matrix products, arithmetic and copies ran while one was open for 6% of the time, Pallas kernels for 0%

commit v1 on v0

--- a/solution.py
+++ b/solution.py
@@ -100,6 +100,175 @@
     return mixed
 
 
+def flip_route(**bits):
+    mask = sum(bits.get(name, 0) << place for place, name in enumerate(("c", "x", "y", "zl", "zh")))
+    return [(i, i ^ mask) for i in range(32)]
+
+
+BOTH = ("ctx", "grp")
+
+
+def flip(block, **bits):
+    return lax.ppermute(block, BOTH, flip_route(**bits))
+
+
+def route(block, rule):
+    pairs = []
+    for i in range(32):
+        zh, zl, y, x, c = [(i >> place) & 1 for place in (4, 3, 2, 1, 0)]
+        there = rule(zh, zl, y, x, c)
+        if there is not None:
+            zh, zl, y, x, c = there
+            pairs.append((i, 16 * zh + 8 * zl + 4 * y + 2 * x + c))
+    return lax.ppermute(block, BOTH, pairs)
+
+
+def ordered(bit, mine, other, axis):
+    return jnp.where(
+        bit == 0,
+        jnp.concatenate([mine, other], axis=axis),
+        jnp.concatenate([other, mine], axis=axis),
+    )
+
+
+def halved(weight, bit):
+    width = weight.shape[1] // 2
+    return lax.dynamic_slice_in_dim(weight, bit * width, width, 1)
+
+
+def gathered(mine, near, far, across, bits):
+    zh, zl, y = bits
+    rows = mine.shape[0]
+    blocks = {(0, 0): mine, (0, 1): near, (1, 0): far, (1, 1): across}
+    whole = jnp.zeros((8 * rows, mine.shape[1]), mine.dtype)
+    first = flip(jnp.concatenate([mine, near], axis=0), y=1)
+    twins = {
+        (0, 0): first[:rows],
+        (0, 1): first[rows:],
+        (1, 0): flip(far, y=1),
+        (1, 1): flip(across, y=1),
+    }
+    for side, group in ((0, blocks), (1, twins)):
+        for (a, b), block in group.items():
+            place = 4 * (zh ^ a) + 2 * (zl ^ b) + (y ^ side)
+            whole = lax.dynamic_update_slice_in_dim(whole, block, place * rows, 0)
+    return whole
+
+
+def halves(q_latent, kv_latent, kv_gain, q_weight, kv_weight, out_weight, documents):
+    rows = q_latent.shape[0]
+    width = q_latent.shape[1]
+    heads = q_weight.shape[1] // (NOPE + ROPE) // 2
+    ctx, grp = lax.axis_index("ctx"), lax.axis_index("grp")
+    zh, zl, y, x, c = ctx // 4, ctx // 2 % 2, ctx % 2, grp // 2, grp % 2
+
+    latents = jnp.concatenate([q_latent, kv_latent], axis=1)
+    latents = lax.dynamic_slice_in_dim(latents, c * (rows // 2), rows // 2, 0)
+    near = flip(latents, zl=1)
+    pair = ordered(zl, latents[None], near[None], 0)
+    kv_pair = pair[:, :, width:]
+    kv_twin = flip(kv_pair, y=1)
+    before = route(
+        kv_pair[1], lambda zh, zl, y, x, c: (1, zl, 0, x, c) if zh == 0 and y == 1 else None
+    )
+    extra = jnp.concatenate([kv_twin, before[None]], axis=0)
+    pair = ordered(c, pair, flip(pair, c=1), 1)
+    extra = ordered(c, extra, flip(extra, c=1), 1)
+    query_in = pair[:, :, :width].reshape(2 * rows, width)
+    own = pair[:, :, width:]
+    prior0 = jnp.where(y == 0, extra[2], extra[0])
+    prior1 = jnp.where(y == 0, extra[0], extra[1])
+    key_in = jnp.concatenate([prior0, own[0], prior1, own[1]], axis=0)
+
+    q_mine, q_other = halved(q_weight, zl), halved(q_weight, 1 - zl)
+    kv_mine, kv_other = halved(kv_weight, zl), halved(kv_weight, 1 - zl)
+    kv_full = gathered(
+        kv_mine,
+        flip(kv_other, zl=1),
+        flip(kv_mine, zh=1),
+        flip(kv_other, zh=1, zl=1),
+        (zh, zl, y),
+    )
+    q_full = gathered(
+        q_mine, flip(q_other, zl=1), flip(q_mine, zh=1), flip(q_other, zh=1, zl=1), (zh, zl, y)
+    )
+
+    blocks = 4 * zh + 2 * jnp.arange(2, dtype=jnp.int32) + y
+    offsets = jnp.arange(rows, dtype=jnp.int32)
+    query_pos = blocks[:, None] * rows + offsets[None, :]
+    key_pos = jnp.concatenate([query_pos - rows, query_pos], axis=1)
+    normed, key_rope = prepare(key_in, key_pos.reshape(-1), kv_gain)
+    key_value = folder(normed, kv_full).astype(jnp.bfloat16)
+    key_value = key_value.reshape(2, 2 * rows, heads, NOPE + VDIM)
+    key_rope = key_rope.reshape(2, 2 * rows, ROPE)
+    query = folder(query_in, q_full).reshape(2 * rows, heads, NOPE + ROPE)
+    query_nope = query[..., :NOPE].astype(jnp.bfloat16).reshape(2, rows, heads, NOPE)
+    query_rope = rotate(query[..., NOPE:], query_pos.reshape(-1)).astype(jnp.bfloat16)
+    query_rope = query_rope.reshape(2, rows, heads, ROPE)
+    query_docs = documents[query_pos]
+    key_docs = documents[jnp.maximum(key_pos, 0)]
+    allowed = (
+        (key_docs[:, None, :] == query_docs[:, :, None])
+        & (key_pos[:, None, :] <= query_pos[:, :, None])
+        & (key_pos[:, None, :] >= 0)
+    )
+    scale = (NOPE + ROPE) ** (-0.5)
+    scores = jnp.einsum(
+        "bqhd,bkhd->bhqk", query_nope, key_value[..., :NOPE], preferred_element_type=jnp.float32
+    )
+    scores = (
+        scores
+        + jnp.einsum("bqhr,bkr->bhqk", query_rope, key_rope, preferred_element_type=jnp.float32)
+    ) * scale
+    scores = jnp.where(allowed[:, None], scores, -1e30)
+    highest = jnp.max(scores, axis=-1, keepdims=True)
+    weights = jnp.exp(scores - highest)
+    probs = (weights / jnp.sum(weights, axis=-1, keepdims=True)).astype(jnp.bfloat16)
+    attended = jnp.einsum(
+        "bhqk,bkhv->bqhv", probs, key_value[..., NOPE:], preferred_element_type=jnp.float32
+    ).astype(jnp.bfloat16)
+    attended = attended.reshape(2 * rows, heads * VDIM)
+
+    near = flip(attended, zl=1)
+    mine = ordered(zl, attended, near, 1)
+    twin = ordered(zl, flip(attended, y=1), flip(near, y=1), 1)
+    columns = out_weight.shape[1]
+    cuts = [(0, columns // 256 * 128), (columns // 256 * 128, columns)]
+    pieces = []
+    for tokens in (mine, twin):
+        tokens = tokens.reshape(2, rows, -1)
+        keep = lax.dynamic_index_in_dim(tokens, c, 0, keepdims=False)
+        give = lax.dynamic_index_in_dim(tokens, 1 - c, 0, keepdims=False)
+        parts = []
+        for begin, end in cuts:
+            chunk = out_weight[:, begin:end]
+            chunk_far = flip(chunk, zh=1)
+            sums = []
+            for weight in (chunk, chunk_far):
+                got = flip(folder(give, weight).astype(jnp.bfloat16), c=1)
+                sums.append(folder(keep, weight) + got.astype(jnp.float32))
+            here, there = sums
+            got_here = route(
+                here.astype(jnp.bfloat16),
+                lambda zh, zl, y, x, c: (zh, zl, y, 1 - x, c) if x != zh else None,
+            )
+            got_there = route(
+                there.astype(jnp.bfloat16),
+                lambda zh, zl, y, x, c: (zh, zl, y, 1 - x, c) if x == zh else None,
+            )
+            parts.append(
+                jnp.where(
+                    x == zh,
+                    here + got_here.astype(jnp.float32),
+                    there + got_there.astype(jnp.float32),
+                ).astype(jnp.bfloat16)
+            )
+        pieces.append(parts)
+    same = [route(p, lambda zh, zl, y, x, c: (zh, c, y, x, zl)) for p in pieces[0]]
+    cross = [route(p, lambda zh, zl, y, x, c: (zh, c, 1 - y, x, zl)) for p in pieces[1]]
+    return ordered(y, jnp.concatenate(same, axis=1), jnp.concatenate(cross, axis=1), 1)
+
+
 def solution(mesh):
     placed = (
         P("ctx", None),
@@ -110,6 +279,7 @@
         P("grp", "ctx"),
         P(),
     )
+    body = halves if (mesh.shape["ctx"], mesh.shape["grp"]) == (8, 4) else per_device
     return jax.shard_map(
-        per_device, mesh=mesh, in_specs=placed, out_specs=P("ctx", "grp"), check_vma=False
-    )
+        body, mesh=mesh, in_specs=placed, out_specs=P("ctx", "grp"), check_vma=False
+    )

time: 401 us -> 320 us (0.80)
  waiting for transfers between devices: 347 us -> 127 us
  local copies, waits for them, and re-layouts: 4.66 us -> 72.8 us
  starting transfers between devices: 5.04 us -> 64.6 us
  other arithmetic: 2.73 us -> 22 us
  between operations: 13.3 us -> 0.89 us
    all_gather x3 -> x0, waiting for transfers between devices: 300 us -> none  [the longest x1 184 us: per_device(): lax.all_gather(out_weight, 'ctx', axis=1, tiled=True)]
    ppermute x1 -> x42, waiting for transfers between devices: 5.22 us -> 127 us  [the longest x29 108 us: flip(): return lax.ppermute(block, BOTH, flip_route(**bits))]
    ppermute x1 -> x42, starting transfers between devices: 4.92 us -> 64.6 us  [the longest x29 39 us: flip(): return lax.ppermute(block, BOTH, flip_route(**bits))]
    dynamic_update_slice x0 -> x17, local copies, waits for them, and re-layouts: none -> 40 us  [gathered(): whole = lax.dynamic_update_slice_in_dim(whole, block, place * rows, 0)]
    reduce_scatter x1 -> x0, waiting for transfers between devices: 39.4 us -> none  [per_device(): lax.psum_scatter(partial_value.astype(jnp.bfloat16), 'grp', scatter_dimen...]
    dot_general x2 -> x18, matrix products: 7.25 us -> 22.3 us  [folder(): return jnp.dot(left, weight_piece, preferred_element_type=jnp.float32)]
    dot_general x4 -> x3, matrix products: 20.8 us -> 9.3 us  [the longest x1 7.57 us: halves(): jnp.einsum('bhqk,bkhv->bqhv', probs, key_value[..., NOPE:], preferred_ele...]
    gather x0 -> x4, local copies, waits for them, and re-layouts: none -> 9.32 us  [the longest x2 6.16 us: halves(): key_docs = documents[jnp.maximum(key_pos, 0)]]
  transfers between devices with their start and end apart: 5 -> 42, of which waited for: 5 -> 15; matrix products, arithmetic and copies ran while one was open for 6% -> 28% of each run, Pallas kernels for 0% -> 0%
where the time goes in v1:
time: 320 us; the launch traced here: 319 us
  waiting for transfers between devices  127 us (40%)
  local copies, waits for them, and re-layouts  72.8 us (23%)
  starting transfers between devices  64.6 us (20%)
  matrix products  31.6 us (10%)
  other arithmetic  22 us (7%)
    ppermute x29, waiting for transfers between devices, flip(): return lax.ppermute(block, BOTH, flip_route(**bits))  108 us
    dynamic_update_slice x17, local copies, waits for them, and re-layouts, gathered(): whole = lax.dynamic_update_slice_in_dim(whole, block, place * rows, 0)  40 us
    ppermute x29, starting transfers between devices, flip(): return lax.ppermute(block, BOTH, flip_route(**bits))  39 us
    ppermute x13, starting transfers between devices, route(): return lax.ppermute(block, BOTH, pairs)  25.7 us
    dot_general x18, matrix products, folder(): return jnp.dot(left, weight_piece, preferred_element_type=jnp.float32)  22.3 us
    ppermute x13, waiting for transfers between devices, route(): return lax.ppermute(block, BOTH, pairs)  18.3 us
    select_n x6, other arithmetic, ordered(): jnp.where(bit == 0, jnp.concatenate([mine, other], axis=axis), jnp.concat...  8.71 us
    dot_general x1, matrix products, halves(): jnp.einsum('bhqk,bkhv->bqhv', probs, key_value[..., NOPE:], preferred_ele...  7.57 us
  transfers between devices with their start and end apart: 42, of which 15 were waited for; matrix products, arithmetic and copies ran while one was open for 28% of the time, Pallas kernels for 0%

profile of v1, /device:TPU:0, one launch (start us, length us, event | category | flops | bytes accessed | tf_op | source)
XLA Modules:
  0.0 318.7 jit_solution(15269538245613034789)
XLA Ops:
  16.4 6.2 %gather_fusion = s32[1024]{0:T(1024)S(1)} fusion(s32[2048]{0:T(1024)S(1)} %copy-done, s32[1024]{0:T(1024)S(1)} %broadcast_clamp_fusion), kind=kCustom, calls=%fused_computation | custom fusion | bytes 12288 | tf_op jit(solution)/shard_map/gather | solution.py:209
  33.6 4.3 %collective-permute-done.6 = bf16[64,1024]{1,0:T(8,128)(2,1)} collective-permute-done((bf16[64,1024]{1,0:T(8,128)(2,1)S(1)}, bf16[64,1024]{1,0:T(8,128)(2,1)}, u32[]{:S(2)}, u32[]{:S(2)}) %collective-permute-start.6) | collective-permute-done | bytes 131104 | tf_op jit(solution)/shard_map/ppermute | solution.py:112
  46.6 7.3 %collective-permute-done.12 = bf16[192,768]{1,0:T(8,128)(2,1)S(1)} collective-permute-done((bf16[192,768]{1,0:T(8,128)(2,1)S(1)}, bf16[192,768]{1,0:T(8,128)(2,1)S(1)}, u32[]{:S(2)}, u32[]{:S(2)}) %collective-permute-start.12) | collective-permute-done | bytes 294944 | tf_op jit(solution)/shard_map/ppermute | solution.py:112
  59.6 4.4 %dynamic_update_slice.59 = bf16[1536,768]{0,1:T(8,128)(2,1)} dynamic-update-slice(bf16[1536,768]{0,1:T(8,128)(2,1)} %copy.44, bf16[192,768]{0,1:T(8,128)(2,1)S(1)} %copy.45, s32[]{:T(128)S(6)} %select_n.237, s32[]{:T(128)} %constant.98.clone.1) | dynamic-update-slice | bytes 589828 | tf_op jit(solution)/shard_map/dynamic_update_slice | solution.py:154
  71.6 5.0 %collective-permute-start.15 = (bf16[192,768]{1,0:T(8,128)(2,1)S(1)}, bf16[192,768]{1,0:T(8,128)(2,1)}, u32[]{:S(2)}, u32[]{:S(2)}) collective-permute-start(bf16[192,768]{1,0:T(8,128)(2,1)S(1)} %copy-done.13), channel_id=1, source_target_pairs={{0,4},{1,5},{2,6},{3,7},{4,0},{5,1},{6,2},{7,3},{8,12},{9,13},{10,... | collective-permute-start | bytes 884744 | tf_op jit(solution)/shard_map/ppermute | solution.py:112
  86.5 4.2 %collective-permute-done.16 = bf16[192,768]{1,0:T(8,128)(2,1)S(1)} collective-permute-done((bf16[192,768]{1,0:T(8,128)(2,1)}, bf16[192,768]{1,0:T(8,128)(2,1)S(1)}, u32[]{:S(2)}, u32[]{:S(2)}) %collective-permute-start.16) | collective-permute-done | bytes 294944 | tf_op jit(solution)/shard_map/ppermute | solution.py:112
  92.3 5.0 %dynamic_update_slice.60 = bf16[1536,768]{0,1:T(8,128)(2,1)} dynamic-update-slice(bf16[1536,768]{0,1:T(8,128)(2,1)} %dynamic_update_slice.59, bf16[192,768]{0,1:T(8,128)(2,1)S(1)} %copy.46, s32[]{:T(128)S(6)} %select_n.238, s32[]{:T(128)} %constant.98.clone.1) | dynamic-update-slice | bytes 589828 | tf_op jit(solution)/shard_map/dynamic_update_slice | solution.py:154
  97.3 5.0 %dynamic_update_slice.61 = bf16[1536,768]{0,1:T(8,128)(2,1)} dynamic-update-slice(bf16[1536,768]{0,1:T(8,128)(2,1)} %dynamic_update_slice.60, bf16[192,768]{0,1:T(8,128)(2,1)S(1)} %copy.47, s32[]{:T(128)S(6)} %select_n.239, s32[]{:T(128)} %constant.98.clone.1) | dynamic-update-slice | bytes 589828 | tf_op jit(solution)/shard_map/dynamic_update_slice | solution.py:154
  102.3 5.1 %dynamic_update_slice.62 = bf16[1536,768]{0,1:T(8,128)(2,1)} dynamic-update-slice(bf16[1536,768]{0,1:T(8,128)(2,1)} %dynamic_update_slice.61, bf16[192,768]{0,1:T(8,128)(2,1)S(1)} %copy.48, s32[]{:T(128)S(6)} %select_n.240, s32[]{:T(128)} %constant.98.clone.1) | dynamic-update-slice | bytes 589828 | tf_op jit(solution)/shard_map/dynamic_update_slice | solution.py:154
  107.4 4.4 %dynamic_update_slice.63 = bf16[1536,768]{0,1:T(8,128)(2,1)} dynamic-update-slice(bf16[1536,768]{0,1:T(8,128)(2,1)} %dynamic_update_slice.62, bf16[192,768]{0,1:T(8,128)(2,1)S(1)} %copy.49, s32[]{:T(128)S(6)} %select_n.241, s32[]{:T(128)} %constant.98.clone.1) | dynamic-update-slice | bytes 589828 | tf_op jit(solution)/shard_map/dynamic_update_slice | solution.py:154
  125.3 3.9 %convolution_convert_fusion = bf16[1024,1024]{1,0:T(8,128)(2,1)} fusion(bf16[512,1024]{1,0:T(8,128)(2,1)} %constant_dynamic-update-slice_fusion.3, f32[512]{0:T(512)S(1)} %copy-done.16, f32[1024]{0:T(1024)S(1)} %add_rsqrt_fusion, bf16[1024,576]{0,1:T(8,128)(2,1)S(1)} %pad_maximum_fusion), kind=kOutput, calls=%fused_computation.15 | convolution fusion | flops 1076887552 | bytes 4200448 | tf_op jit(solution)/shard_map/dot_general | solution.py:46
  140.3 7.6 %fusion.7 = bf16[2,4,128,256]{3,2,1,0:T(8,128)(2,1)S(1)} fusion(f32[2,4,256]{2,1,0:T(4,128)S(1)} %fusion.114, bf16[2,512,4,128]{3,2,1,0:T(4,128)(2,1)S(1)} %copy-done.8, f32[2,4,256,512]{3,2,1,0:T(8,128)} %copy-done.2), kind=kOutput, calls=%fused_computation.16 | convolution fusion | flops 271845888 | bytes 5775360 | tf_op jit(solution)/shard_map/bhqk,bkhv->bqhv/dot_general | solution.py:227
  149.1 4.2 %collective-permute-start.17 = (bf16[512,512]{1,0:T(8,128)(2,1)}, bf16[512,512]{1,0:T(8,128)(2,1)}, u32[]{:S(2)}, u32[]{:S(2)}) collective-permute-start(bf16[512,512]{1,0:T(8,128)(2,1)} %bitcast.147), channel_id=1, source_target_pairs={{0,8},{1,9},{2,10},{3,11},{4,12},{5,13},{6,14},{7,15},{8,0},{9,1},... | collective-permute-start | bytes 1572872 | tf_op jit(solution)/shard_map/ppermute | solution.py:112
  154.2 4.6 %collective-permute-start.20 = (bf16[1024,384]{1,0:T(8,128)(2,1)}, bf16[1024,384]{1,0:T(8,128)(2,1)}, u32[]{:S(2)}, u32[]{:S(2)}) collective-permute-start(bf16[1024,384]{1,0:T(8,128)(2,1)} %slice.101), channel_id=1, source_target_pairs={{0,16},{1,17},{2,18},{3,19},{4,20},{5,21},{6,22},{7,23},{8,24},{9,... | collective-permute-start | bytes 2359304 | tf_op jit(solution)/shard_map/ppermute | solution.py:112
  161.1 14.1 %collective-permute-done.17 = bf16[512,512]{1,0:T(8,128)(2,1)} collective-permute-done((bf16[512,512]{1,0:T(8,128)(2,1)}, bf16[512,512]{1,0:T(8,128)(2,1)}, u32[]{:S(2)}, u32[]{:S(2)}) %collective-permute-start.17) | collective-permute-done | bytes 524320 | tf_op jit(solution)/shard_map/ppermute | solution.py:112
  177.3 39.5 %collective-permute-done.20 = bf16[1024,384]{1,0:T(8,128)(2,1)} collective-permute-done((bf16[1024,384]{1,0:T(8,128)(2,1)}, bf16[1024,384]{1,0:T(8,128)(2,1)}, u32[]{:S(2)}, u32[]{:S(2)}) %collective-permute-start.20) | collective-permute-done | bytes 786464 | tf_op jit(solution)/shard_map/ppermute | solution.py:112
  219.5 17.9 %collective-permute-done.26 = bf16[1024,512]{1,0:T(8,128)(2,1)S(1)} collective-permute-done((bf16[1024,512]{1,0:T(8,128)(2,1)}, bf16[1024,512]{1,0:T(8,128)(2,1)S(1)}, u32[]{:S(2)}, u32[]{:S(2)}) %collective-permute-start.26) | collective-permute-done | bytes 1048608 | tf_op jit(solution)/shard_map/ppermute | solution.py:112
  242.9 5.9 %collective-permute-start.22 = (bf16[256,384]{1,0:T(8,128)(2,1)}, bf16[256,384]{1,0:T(8,128)(2,1)}, u32[]{:S(2)}, u32[]{:S(2)}) collective-permute-start(bf16[256,384]{1,0:T(8,128)(2,1)} %get-tuple-element.44), channel_id=1, source_target_pairs={{0,2},{1,3},{4,6},{5,7},{8,10},{9,11},{12,14},{13,15},{18,16},{19,... | collective-permute-start | bytes 589832 | tf_op jit(solution)/shard_map/ppermute | solution.py:123
  252.6 5.9 %collective-permute-start.28 = (bf16[256,512]{1,0:T(8,128)(2,1)}, bf16[256,512]{1,0:T(8,128)(2,1)}, u32[]{:S(2)}, u32[]{:S(2)}) collective-permute-start(bf16[256,512]{1,0:T(8,128)(2,1)} %get-tuple-element.40), channel_id=1, source_target_pairs={{0,2},{1,3},{4,6},{5,7},{8,10},{9,11},{12,14},{13,15},{18,16},{19,... | collective-permute-start | bytes 786440 | tf_op jit(solution)/shard_map/ppermute | solution.py:123
  265.5 8.0 %collective-permute-done.30 = bf16[512,512]{1,0:T(8,128)(2,1)S(1)} collective-permute-done((bf16[512,512]{1,0:T(8,128)(2,1)}, bf16[512,512]{1,0:T(8,128)(2,1)S(1)}, u32[]{:S(2)}, u32[]{:S(2)}) %collective-permute-start.30) | collective-permute-done | bytes 524320 | tf_op jit(solution)/shard_map/ppermute | solution.py:112
  273.5 9.6 %collective-permute-done.31 = bf16[512,512]{1,0:T(8,128)(2,1)S(1)} collective-permute-done((bf16[512,512]{1,0:T(8,128)(2,1)}, bf16[512,512]{1,0:T(8,128)(2,1)S(1)}, u32[]{:S(2)}, u32[]{:S(2)}) %collective-permute-start.31) | collective-permute-done | bytes 524320 | tf_op jit(solution)/shard_map/ppermute | solution.py:112
  291.6 4.6 %collective-permute-start.40 = (bf16[256,512]{1,0:T(8,128)(2,1)S(1)}, bf16[256,512]{1,0:T(8,128)(2,1)S(1)}, u32[]{:S(2)}, u32[]{:S(2)}) collective-permute-start(bf16[256,512]{1,0:T(8,128)(2,1)S(1)} %get-tuple-element.32), channel_id=1, source_target_pairs={{0,2},{1,3},{4,6},{5,7},{8,10},{9,11},{12,14},{13,15},{18,16},{19,... | collective-permute-start | bytes 786440 | tf_op jit(solution)/shard_map/ppermute | solution.py:123
  297.8 4.9 %collective-permute-done.38 = bf16[256,512]{1,0:T(8,128)(2,1)S(1)} collective-permute-done((bf16[256,512]{1,0:T(8,128)(2,1)S(1)}, bf16[256,512]{1,0:T(8,128)(2,1)S(1)}, u32[]{:S(2)}, u32[]{:S(2)}) %collective-permute-start.38) | collective-permute-done | bytes 262176 | tf_op jit(solution)/shard_map/ppermute | solution.py:123
  308.4 9.1 %collective-permute-done.36 = bf16[256,384]{1,0:T(8,128)(2,1)S(1)} collective-permute-done((bf16[256,384]{1,0:T(8,128)(2,1)S(1)}, bf16[256,384]{1,0:T(8,128)(2,1)S(1)}, u32[]{:S(2)}, u32[]{:S(2)}) %collective-permute-start.36) | collective-permute-done | bytes 196640 | tf_op jit(solution)/shard_map/ppermute | solution.py:123
  (198 shorter events, 127.2 us)
Async XLA Ops:
  2.0 44.1 %collective-permute-start.11 = (bf16[192,768]{1,0:T(8,128)(2,1)}, bf16[192,768]{1,0:T(8,128)(2,1)S(1)}, u32[]{:S(2)}, u32[]{:S(2)}) collective-permute-start(bf16[192,768]{1,0:T(8,128)(2,1)} %get-tuple-element.19), channel_id=1, source_target_pairs={{0,8},{1,9},{2,10},{3,11},{4,12},{5,13},{6,14},{7,15},{8,0},{9,1},... | collective-permute-start | bytes 884744 | tf_op jit(solution)/shard_map/ppermute | solution.py:112
  5.1 52.9 %collective-permute-start.13 = (bf16[192,768]{1,0:T(8,128)(2,1)}, bf16[192,768]{1,0:T(8,128)(2,1)}, u32[]{:S(2)}, u32[]{:S(2)}) collective-permute-start(bf16[192,768]{1,0:T(8,128)(2,1)} %get-tuple-element.19), channel_id=1, source_target_pairs={{0,24},{1,25},{2,26},{3,27},{4,28},{5,29},{6,30},{7,31},{8,16},{9,... | collective-permute-start | bytes 884744 | tf_op jit(solution)/shard_map/ppermute | solution.py:112
  10.4 17.4 %collective-permute-start.5 = (bf16[64,1024]{1,0:T(8,128)(2,1)}, bf16[64,1024]{1,0:T(8,128)(2,1)}, u32[]{:S(2)}, u32[]{:S(2)}) collective-permute-start(bf16[64,1024]{1,0:T(8,128)(2,1)} %get-tuple-element.22), channel_id=1, source_target_pairs={{0,8},{1,9},{2,10},{3,11},{4,12},{5,13},{6,14},{7,15},{8,0},{9,1},... | collective-permute-start | bytes 393224 | tf_op jit(solution)/shard_map/ppermute | solution.py:112
  11.1 31.8 %collective-permute-start.7 = (bf16[64,1024]{1,0:T(8,128)(2,1)}, bf16[64,1024]{1,0:T(8,128)(2,1)}, u32[]{:S(2)}, u32[]{:S(2)}) collective-permute-start(bf16[64,1024]{1,0:T(8,128)(2,1)} %get-tuple-element.22), channel_id=1, source_target_pairs={{0,24},{1,25},{2,26},{3,27},{4,28},{5,29},{6,30},{7,31},{8,16},{9,... | collective-permute-start | bytes 393224 | tf_op jit(solution)/shard_map/ppermute | solution.py:112
  15.2 50.4 %collective-permute-start = (bf16[128,2112]{0,1:T(8,128)(2,1)}, bf16[128,2112]{0,1:T(8,128)(2,1)}, u32[]{:S(2)}, u32[]{:S(2)}) collective-permute-start(bf16[128,2112]{0,1:T(8,128)(2,1)} %fusion.15), channel_id=1, source_target_pairs={{0,8},{1,9},{2,10},{3,11},{4,12},{5,13},{6,14},{7,15},{8,0},{9,1},... | collective-permute-start | bytes 1622024 | tf_op jit(solution)/shard_map/ppermute | solution.py:112
  37.9 16.0 %collective-permute-start.12 = (bf16[192,768]{1,0:T(8,128)(2,1)S(1)}, bf16[192,768]{1,0:T(8,128)(2,1)S(1)}, u32[]{:S(2)}, u32[]{:S(2)}) collective-permute-start(bf16[192,768]{1,0:T(8,128)(2,1)S(1)} %copy-done.6), channel_id=1, source_target_pairs={{0,16},{1,17},{2,18},{3,19},{4,20},{5,21},{6,22},{7,23},{8,24},{9,... | collective-permute-start | bytes 884744 | tf_op jit(solution)/shard_map/ppermute | solution.py:112
  43.0 21.1 %collective-permute-start.8 = (bf16[128,1024]{1,0:T(8,128)(2,1)}, bf16[128,1024]{1,0:T(8,128)(2,1)}, u32[]{:S(2)}, u32[]{:S(2)}) collective-permute-start(bf16[128,1024]{1,0:T(8,128)(2,1)} %pad_maximum_fusion.3), channel_id=1, source_target_pairs={{0,4},{1,5},{2,6},{3,7},{4,0},{5,1},{6,2},{7,3},{8,12},{9,13},{10,... | collective-permute-start | bytes 786440 | tf_op jit(solution)/shard_map/ppermute | solution.py:112
  46.1 23.3 %collective-permute-start.9 = (bf16[64,1024]{1,0:T(8,128)(2,1)}, bf16[64,1024]{1,0:T(8,128)(2,1)}, u32[]{:S(2)}, u32[]{:S(2)}) collective-permute-start(bf16[64,1024]{1,0:T(8,128)(2,1)} %collective-permute-done.6), channel_id=1, source_target_pairs={{0,4},{1,5},{2,6},{3,7},{4,0},{5,1},{6,2},{7,3},{8,12},{9,13},{10,... | collective-permute-start | bytes 393224 | tf_op jit(solution)/shard_map/ppermute | solution.py:112
  53.9 27.1 %collective-permute-start.10 = (bf16[64,1024]{1,0:T(8,128)(2,1)}, bf16[64,1024]{1,0:T(8,128)(2,1)}, u32[]{:S(2)}, u32[]{:S(2)}) collective-permute-start(bf16[64,1024]{1,0:T(8,128)(2,1)} %collective-permute-done.7), channel_id=1, source_target_pairs={{0,4},{1,5},{2,6},{3,7},{4,0},{5,1},{6,2},{7,3},{8,12},{9,13},{10,... | collective-permute-start | bytes 393224 | tf_op jit(solution)/shard_map/ppermute | solution.py:112
  57.9 32.9 %collective-permute-start.14 = (bf16[384,768]{1,0:T(8,128)(2,1)S(1)}, bf16[384,768]{1,0:T(8,128)(2,1)}, u32[]{:S(2)}, u32[]{:S(2)}) collective-permute-start(bf16[384,768]{1,0:T(8,128)(2,1)S(1)} %pad_maximum_fusion.1), channel_id=1, source_target_pairs={{0,4},{1,5},{2,6},{3,7},{4,0},{5,1},{6,2},{7,3},{8,12},{9,13},{10,... | collective-permute-start | bytes 1769480 | tf_op jit(solution)/shard_map/ppermute | solution.py:112
  69.2 44.1 %collective-permute-start.4 = (bf16[2,128,2112]{1,2,0:T(8,128)(2,1)S(1)}, bf16[2,128,2112]{1,2,0:T(8,128)(2,1)}, u32[]{:S(2)}, u32[]{:S(2)}) collective-permute-start(bf16[2,128,2112]{1,2,0:T(8,128)(2,1)S(1)} %maximum_select_fusion.1), channel_id=1, source_target_pairs={{0,1},{1,0},{2,3},{3,2},{4,5},{5,4},{6,7},{7,6},{8,9},{9,8},{10,11... | collective-permute-start | bytes 3244040 | tf_op jit(solution)/shard_map/ppermute | solution.py:112
  81.0 30.7 %collective-permute-start.3 = (bf16[3,128,576]{1,2,0:T(8,128)(2,1)}, bf16[3,128,576]{1,2,0:T(8,128)(2,1)}, u32[]{:S(2)}, u32[]{:S(2)}) collective-permute-start(bf16[3,128,576]{1,2,0:T(8,128)(2,1)} %pad_maximum_fusion.2), channel_id=1, source_target_pairs={{0,1},{1,0},{2,3},{3,2},{4,5},{5,4},{6,7},{7,6},{8,9},{9,8},{10,11... | collective-permute-start | bytes 1327112 | tf_op jit(solution)/shard_map/ppermute | solution.py:112
  149.1 26.1 %collective-permute-start.17 = (bf16[512,512]{1,0:T(8,128)(2,1)}, bf16[512,512]{1,0:T(8,128)(2,1)}, u32[]{:S(2)}, u32[]{:S(2)}) collective-permute-start(bf16[512,512]{1,0:T(8,128)(2,1)} %bitcast.147), channel_id=1, source_target_pairs={{0,8},{1,9},{2,10},{3,11},{4,12},{5,13},{6,14},{7,15},{8,0},{9,1},... | collective-permute-start | bytes 1572872 | tf_op jit(solution)/shard_map/ppermute | solution.py:112
  154.2 62.6 %collective-permute-start.20 = (bf16[1024,384]{1,0:T(8,128)(2,1)}, bf16[1024,384]{1,0:T(8,128)(2,1)}, u32[]{:S(2)}, u32[]{:S(2)}) collective-permute-start(bf16[1024,384]{1,0:T(8,128)(2,1)} %slice.101), channel_id=1, source_target_pairs={{0,16},{1,17},{2,18},{3,19},{4,20},{5,21},{6,22},{7,23},{8,24},{9,... | collective-permute-start | bytes 2359304 | tf_op jit(solution)/shard_map/ppermute | solution.py:112
  159.8 77.5 %collective-permute-start.26 = (bf16[1024,512]{1,0:T(8,128)(2,1)}, bf16[1024,512]{1,0:T(8,128)(2,1)S(1)}, u32[]{:S(2)}, u32[]{:S(2)}) collective-permute-start(bf16[1024,512]{1,0:T(8,128)(2,1)} %slice.102), channel_id=1, source_target_pairs={{0,16},{1,17},{2,18},{3,19},{4,20},{5,21},{6,22},{7,23},{8,24},{9,... | collective-permute-start | bytes 3145736 | tf_op jit(solution)/shard_map/ppermute | solution.py:112
  177.2 60.7 %collective-permute-start.18 = (bf16[256,384]{1,0:T(8,128)(2,1)S(1)}, bf16[256,384]{1,0:T(8,128)(2,1)S(1)}, u32[]{:S(2)}, u32[]{:S(2)}) collective-permute-start(bf16[256,384]{1,0:T(8,128)(2,1)S(1)} %convolution_convert_fusion.8), channel_id=1, source_target_pairs={{0,1},{1,0},{2,3},{3,2},{4,5},{5,4},{6,7},{7,6},{8,9},{9,8},{10,11... | collective-permute-start | bytes 589832 | tf_op jit(solution)/shard_map/ppermute | solution.py:112
  218.4 22.1 %collective-permute-start.21 = (bf16[256,384]{1,0:T(8,128)(2,1)S(1)}, bf16[256,384]{1,0:T(8,128)(2,1)S(1)}, u32[]{:S(2)}, u32[]{:S(2)}) collective-permute-start(bf16[256,384]{1,0:T(8,128)(2,1)S(1)} %convolution_convert_fusion.7), channel_id=1, source_target_pairs={{0,1},{1,0},{2,3},{3,2},{4,5},{5,4},{6,7},{7,6},{8,9},{9,8},{10,11... | collective-permute-start | bytes 589832 | tf_op jit(solution)/shard_map/ppermute | solution.py:112
  218.9 29.9 %collective-permute-start.24 = (bf16[256,512]{1,0:T(8,128)(2,1)S(1)}, bf16[256,512]{1,0:T(8,128)(2,1)S(1)}, u32[]{:S(2)}, u32[]{:S(2)}) collective-permute-start(bf16[256,512]{1,0:T(8,128)(2,1)S(1)} %convolution_convert_fusion.4), channel_id=1, source_target_pairs={{0,1},{1,0},{2,3},{3,2},{4,5},{5,4},{6,7},{7,6},{8,9},{9,8},{10,11... | collective-permute-start | bytes 786440 | tf_op jit(solution)/shard_map/ppermute | solution.py:112
  239.2 19.3 %collective-permute-start.19 = (bf16[256,384]{1,0:T(8,128)(2,1)}, bf16[256,384]{1,0:T(8,128)(2,1)}, u32[]{:S(2)}, u32[]{:S(2)}) collective-permute-start(bf16[256,384]{1,0:T(8,128)(2,1)} %get-tuple-element.46), channel_id=1, source_target_pairs={{2,0},{3,1},{6,4},{7,5},{10,8},{11,9},{14,12},{15,13},{16,18},{17,... | collective-permute-start | bytes 589832 | tf_op jit(solution)/shard_map/ppermute | solution.py:123
  242.9 17.6 %collective-permute-start.22 = (bf16[256,384]{1,0:T(8,128)(2,1)}, bf16[256,384]{1,0:T(8,128)(2,1)}, u32[]{:S(2)}, u32[]{:S(2)}) collective-permute-start(bf16[256,384]{1,0:T(8,128)(2,1)} %get-tuple-element.44), channel_id=1, source_target_pairs={{0,2},{1,3},{4,6},{5,7},{8,10},{9,11},{12,14},{13,15},{18,16},{19,... | collective-permute-start | bytes 589832 | tf_op jit(solution)/shard_map/ppermute | solution.py:123
  258.5 24.6 %collective-permute-start.31 = (bf16[512,512]{1,0:T(8,128)(2,1)}, bf16[512,512]{1,0:T(8,128)(2,1)S(1)}, u32[]{:S(2)}, u32[]{:S(2)}) collective-permute-start(bf16[512,512]{1,0:T(8,128)(2,1)} %collective-permute-done.17), channel_id=1, source_target_pairs={{0,4},{1,5},{2,6},{3,7},{4,0},{5,1},{6,2},{7,3},{8,12},{9,13},{10,... | collective-permute-start | bytes 1572872 | tf_op jit(solution)/shard_map/ppermute | solution.py:112
  261.9 46.5 %collective-permute-start.23 = (bf16[256,384]{1,0:T(8,128)(2,1)S(1)}, bf16[256,384]{1,0:T(8,128)(2,1)S(1)}, u32[]{:S(2)}, u32[]{:S(2)}) collective-permute-start(bf16[256,384]{1,0:T(8,128)(2,1)S(1)} %select_convert_fusion.3), channel_id=1, source_target_pairs={{0,0},{1,8},{2,2},{3,10},{4,4},{5,12},{6,6},{7,14},{8,1},{9,9},{10... | collective-permute-start | bytes 589832 | tf_op jit(solution)/shard_map/ppermute | solution.py:123
  264.8 43.6 %collective-permute-start.29 = (bf16[256,512]{1,0:T(8,128)(2,1)S(1)}, bf16[256,512]{1,0:T(8,128)(2,1)S(1)}, u32[]{:S(2)}, u32[]{:S(2)}) collective-permute-start(bf16[256,512]{1,0:T(8,128)(2,1)S(1)} %select_convert_fusion.1), channel_id=1, source_target_pairs={{0,0},{1,8},{2,2},{3,10},{4,4},{5,12},{6,6},{7,14},{8,1},{9,9},{10... | collective-permute-start | bytes 786440 | tf_op jit(solution)/shard_map/ppermute | solution.py:123
  288.1 16.6 %collective-permute-start.33 = (bf16[256,384]{1,0:T(8,128)(2,1)S(1)}, bf16[256,384]{1,0:T(8,128)(2,1)S(1)}, u32[]{:S(2)}, u32[]{:S(2)}) collective-permute-start(bf16[256,384]{1,0:T(8,128)(2,1)S(1)} %get-tuple-element.38), channel_id=1, source_target_pairs={{2,0},{3,1},{6,4},{7,5},{10,8},{11,9},{14,12},{15,13},{16,18},{17,... | collective-permute-start | bytes 589832 | tf_op jit(solution)/shard_map/ppermute | solution.py:123
  (36 other events, 267.4 us)
